TPU v7x, 512 devices: a 4x2x32 block of a 4x8x32 slice. The times are simulated.
512 devices in a mesh: parts: 2 (over y), pix: 32 (over z), par: 8 (over x, core).
Axes of the slice: x: 4, y: 2, z: 32, core: 2. Of those that a mesh axis runs over, the one named last changes fastest.
The devices are a block of a 4x8x32 slice.
Arguments:
- green_matrix: bfloat16 [36864, 16384], P('pix', 'par'), may hold values from -0.046875 to 0.046875
- observed: bfloat16 [64, 36864], P('parts', 'pix'), parts along dimension 0, may hold values from -1000 to 1000
Outputs:
- solution: float32 [64, 16384], P('parts', 'par'), parts along dimension 0
- residual: float32 [64, 36864], P('parts', 'pix'), parts along dimension 0
There are 2 independent parts, one for each index of `parts`. A program takes and returns all parts, laid end to end along the dimension named above; an argument that names none is the same for every part. Nothing has to cross between parts.
All inputs are finite; a program needn't handle non-finite values.
Results may differ from a plain program's by a relative error of at most 0.0038.
Values may be sent and summed in bfloat16 or wider, within the bound.
A program may use at most 64 MiB of HBM per device.

v0:
```python
import functools

import jax
import jax.numpy as jnp
from jax import lax
from jax.sharding import Mesh
from jax.sharding import PartitionSpec as P

GRID = 128
ITERS = 5
PAR = ("par_0", "par_1")
PIX_PAR = ("pix", "par_0", "par_1")


def padded_2(block, sides, width):
    for axis, dim in sides:
        count = lax.axis_size(axis)
        forward = [(i, i + 1) for i in range(count - 1)]
        backward = [(target, source) for source, target in forward]
        low = lax.ppermute(
            lax.slice_in_dim(block, block.shape[dim] - width, None, axis=dim), axis, forward
        )
        high = lax.ppermute(lax.slice_in_dim(block, 0, width, axis=dim), axis, backward)
        block = jnp.concatenate([low, block, high], axis=dim)
    return block


def sent_to_all(shard, axis):
    copies = jnp.broadcast_to(shard, (lax.axis_size(axis), *shard.shape))
    return lax.all_to_all(copies, axis, split_axis=0, concat_axis=0, tiled=True)


def taken_together(shard, axis):
    return sent_to_all(shard, axis).sum(axis=0)


def cut_along(shard, dim, length):
    dims = shard.shape
    parts = shard.reshape(*dims[:dim], length, dims[dim] // length, *dims[dim + 1 :])
    return jnp.moveaxis(parts, dim, 0)


def sum_at_owner(shard, axis, dim):
    length = lax.axis_size(axis)
    parts = lax.all_to_all(cut_along(shard, dim, length), axis, 0, 0, tiled=True)
    return jnp.sum(parts, axis=0)


def by_axis(shard, axes):
    return functools.reduce(lax.psum, axes, shard)


def joined_along(parts, dim):
    parts = jnp.moveaxis(parts, 0, dim)
    dims = parts.shape
    return parts.reshape(*dims[:dim], dims[dim] * dims[dim + 1], *dims[dim + 2 :])


def collect(shard, axis, dim):
    parts = sent_to_all(shard, axis)
    return joined_along(parts, dim)


def smooth(values):
    set_count = values.shape[0]
    grid_rows = values.shape[1] // GRID
    tiles = values.reshape(set_count, grid_rows, GRID)
    padded = padded_2(tiles, ((PAR, 1),), 1)
    padded = jnp.pad(padded, ((0, 0), (0, 0), (1, 1)))
    beside_all = (
        padded[:, 2:, 1:-1] + padded[:, :-2, 1:-1] + padded[:, 1:-1, 2:] + padded[:, 1:-1, :-2]
    )
    return (0.25 * (4.0 * tiles - beside_all)).reshape(set_count, grid_rows * GRID)


def forward(rounded, green_matrix):
    partial_value = lax.dot_general(
        rounded, green_matrix, (((1,), (1,)), ((), ())), preferred_element_type=jnp.float32
    )
    return taken_together(partial_value, PAR)


def curvatures(image, smoothed):
    local_image = jnp.sum(image * image, axis=1)
    local_smooth = jnp.sum(smoothed * smoothed, axis=1)
    image_sq = taken_together(local_image, "pix")
    smooth_sq = taken_together(local_smooth, PAR)
    return image_sq + smooth_sq


def on_device(green_matrix, observed):
    set_count = observed.shape[0]
    tile_cells = green_matrix.shape[1]
    residual = observed.astype(jnp.float32)
    share_rows = set_count // lax.axis_size("pix")
    share_start = lax.axis_index("pix") * share_rows

    def backward_rows(rounded_res):
        return sum_at_owner(
            jnp.dot(rounded_res, green_matrix, preferred_element_type=jnp.float32), "pix", 0
        )

    def share_squares(gradient):
        local_sq = jnp.sum(gradient * gradient, axis=1)
        full_sq = lax.dynamic_update_slice_in_dim(
            jnp.zeros((set_count,), jnp.float32), local_sq, share_start, 0
        )
        return by_axis(full_sq, PIX_PAR)

    gradient = backward_rows(observed)
    grad_sq = share_squares(gradient)
    direction = gradient
    solution = jnp.zeros((share_rows, tile_cells), jnp.float32)
    smooth_res = jnp.zeros((share_rows, tile_cells), jnp.float32)
    for sweep in range(ITERS):
        rounded = collect(direction.astype(jnp.bfloat16), "pix", 0)
        image = forward(rounded, green_matrix)
        smoothed_all = smooth(lax.optimization_barrier(rounded).astype(jnp.float32))
        step_all = grad_sq / curvatures(image, smoothed_all)
        step_share = lax.dynamic_slice_in_dim(step_all, share_start, share_rows, 0)[:, None]
        smoothed = lax.dynamic_slice_in_dim(smoothed_all, share_start, share_rows, 0)
        solution = solution + step_share * direction
        residual = residual - step_all[:, None] * image
        smooth_res = smooth_res - step_share * smoothed
        if sweep + 1 < ITERS:
            gradient = backward_rows(residual.astype(jnp.bfloat16)) + smooth(smooth_res)
            fresh_sq = share_squares(gradient)
            ratio_share = lax.dynamic_slice_in_dim(fresh_sq / grad_sq, share_start, share_rows, 0)
            direction = gradient + ratio_share[:, None] * direction
            grad_sq = fresh_sq
    solution = collect(solution, "pix", 0)
    return (solution, residual)


def solution(mesh):
    finer = Mesh(
        mesh.devices.reshape(mesh.shape["parts"], mesh.shape["pix"], 4, 2),
        ("parts", "pix", "par_0", "par_1"),
    )
    placed = (P("pix", PAR), P("parts", "pix"))
    return jax.shard_map(
        on_device,
        mesh=finer,
        in_specs=placed,
        out_specs=(P("parts", PAR), P("parts", "pix")),
        check_vma=False,
    )
```

profile of v0, /device:TPU:33, one launch (start us, length us, event | category | flops | bytes accessed | tf_op | source)
XLA Modules:
  0.0 1180.0 jit_solution(16703593896039843316)
XLA Ops:
  4.9 46.3 %all-to-all-start = ((f32[32,1,2048]{2,1,0:T(1,128)}), f32[32,1,2048]{2,1,0:T(1,128)S(1)}, u32[]{:S(2)}, u32[]{:S(2)}) async-start(f32[32,1,2048]{2,1,0:T(1,128)} %copy.19), calls=%async_computation | async-start | bytes 524288 | tf_op jit(solution)/shard_map/all_to_all | solution.py:45
  51.2 41.0 %all-to-all-done = f32[32,1,2048]{2,1,0:T(1,128)S(1)} async-done(((f32[32,1,2048]{2,1,0:T(1,128)}), f32[32,1,2048]{2,1,0:T(1,128)S(1)}, u32[]{:S(2)}, u32[]{:S(2)}) %all-to-all-start) | async-done | bytes 262176 | tf_op jit(solution)/shard_map/all_to_all | solution.py:45
  95.1 32.0 %all_to_all.140 = bf16[32,2,1024]{2,1,0:T(2,128)(2,1)S(1)} all-to-all(bf16[32,2,1024]{2,1,0:T(2,128)(2,1)S(1)} %reshape.413), channel_id=1, replica_groups=mesh['parts'=2,'pix'=32,'par_0'=4,'par_1'=2] {'pix'}, dimensions={0} | all-to-all | bytes 262144 | tf_op jit(solution)/shard_map/all_to_all | solution.py:30
  172.4 43.9 %psum.105 = f32[32]{0:T(128)S(1)} all-reduce(f32[32]{0:T(128)S(1)} %dynamic_update_slice.15), channel_id=1, replica_groups=mesh['parts'=2,'pix'=32,'par_0'=4,'par_1'=2] {'pix'}, use_global_device_ids=true, to_apply=%region_2.0 | all-reduce | flops 32 | bytes 256 | tf_op jit(solution)/shard_map/psum | solution.py:50
  271.4 33.6 %all-to-all-done.5 = f32[32,1,2048]{2,1,0:T(1,128)S(1)} async-done(((f32[32,1,2048]{2,1,0:T(1,128)}), f32[32,1,2048]{2,1,0:T(1,128)S(1)}, u32[]{:S(2)}, u32[]{:S(2)}) %all-to-all-start.5) | async-done | bytes 262176 | tf_op jit(solution)/shard_map/all_to_all | solution.py:45
  306.6 38.9 %psum.108 = f32[32]{0:T(128)S(1)} all-reduce(f32[32]{0:T(128)S(1)} %dynamic_update_slice.16), channel_id=1, replica_groups=mesh['parts'=2,'pix'=32,'par_0'=4,'par_1'=2] {'pix'}, use_global_device_ids=true, to_apply=%region_12.13 | all-reduce | flops 32 | bytes 256 | tf_op jit(solution)/shard_map/psum | solution.py:50
  374.8 35.4 %all_to_all.141 = bf16[32,2,1024]{2,1,0:T(2,128)(2,1)S(1)} all-to-all(bf16[32,2,1024]{2,1,0:T(2,128)(2,1)S(1)} %reshape.415), channel_id=1, replica_groups=mesh['parts'=2,'pix'=32,'par_0'=4,'par_1'=2] {'pix'}, dimensions={0} | all-to-all | bytes 262144 | tf_op jit(solution)/shard_map/all_to_all | solution.py:30
  452.7 20.4 %all-to-all-done.8 = f32[32,1,32]{2,1,0:T(1,128)S(1)} async-done(((f32[32,1,32]{2,1,0:T(1,128)}), f32[32,1,32]{2,1,0:T(1,128)S(1)}, u32[]{:S(2)}, u32[]{:S(2)}) %all-to-all-start.8) | async-done | bytes 4128 | tf_op jit(solution)/shard_map/all_to_all | solution.py:30
  491.2 29.2 %all-to-all-done.10 = f32[32,1,2048]{2,1,0:T(1,128)S(1)} async-done(((f32[32,1,2048]{2,1,0:T(1,128)}), f32[32,1,2048]{2,1,0:T(1,128)S(1)}, u32[]{:S(2)}, u32[]{:S(2)}) %all-to-all-start.10) | async-done | bytes 262176 | tf_op jit(solution)/shard_map/all_to_all | solution.py:45
  522.0 40.2 %psum.111 = f32[32]{0:T(128)S(1)} all-reduce(f32[32]{0:T(128)S(1)} %dynamic_update_slice.17), channel_id=1, replica_groups=mesh['parts'=2,'pix'=32,'par_0'=4,'par_1'=2] {'pix'}, use_global_device_ids=true, to_apply=%region_22.23 | all-reduce | flops 32 | bytes 256 | tf_op jit(solution)/shard_map/psum | solution.py:50
  569.1 21.7 %psum.113 = f32[32]{0:T(128)S(1)} all-reduce(f32[32]{0:T(128)S(1)} %psum.112), channel_id=1, replica_groups=mesh['parts'=2,'pix'=32,'par_0'=4,'par_1'=2] {'par_1'}, use_global_device_ids=true, to_apply=%region_24.25 | all-reduce | flops 32 | bytes 256 | tf_op jit(solution)/shard_map/psum | solution.py:50
  593.7 35.7 %all_to_all.142 = bf16[32,2,1024]{2,1,0:T(2,128)(2,1)S(1)} all-to-all(bf16[32,2,1024]{2,1,0:T(2,128)(2,1)S(1)} %reshape.417), channel_id=1, replica_groups=mesh['parts'=2,'pix'=32,'par_0'=4,'par_1'=2] {'pix'}, dimensions={0} | all-to-all | bytes 262144 | tf_op jit(solution)/shard_map/all_to_all | solution.py:30
  672.0 20.4 %all-to-all-done.13 = f32[32,1,32]{2,1,0:T(1,128)S(1)} async-done(((f32[32,1,32]{2,1,0:T(1,128)}), f32[32,1,32]{2,1,0:T(1,128)S(1)}, u32[]{:S(2)}, u32[]{:S(2)}) %all-to-all-start.13) | async-done | bytes 4128 | tf_op jit(solution)/shard_map/all_to_all | solution.py:30
  709.8 29.8 %all-to-all-done.15 = f32[32,1,2048]{2,1,0:T(1,128)S(1)} async-done(((f32[32,1,2048]{2,1,0:T(1,128)}), f32[32,1,2048]{2,1,0:T(1,128)S(1)}, u32[]{:S(2)}, u32[]{:S(2)}) %all-to-all-start.15) | async-done | bytes 262176 | tf_op jit(solution)/shard_map/all_to_all | solution.py:45
  741.3 40.2 %psum.114 = f32[32]{0:T(128)S(1)} all-reduce(f32[32]{0:T(128)S(1)} %dynamic_update_slice.18), channel_id=1, replica_groups=mesh['parts'=2,'pix'=32,'par_0'=4,'par_1'=2] {'pix'}, use_global_device_ids=true, to_apply=%region_32.33 | all-reduce | flops 32 | bytes 256 | tf_op jit(solution)/shard_map/psum | solution.py:50
  788.4 21.8 %psum.116 = f32[32]{0:T(128)S(1)} all-reduce(f32[32]{0:T(128)S(1)} %psum.115), channel_id=1, replica_groups=mesh['parts'=2,'pix'=32,'par_0'=4,'par_1'=2] {'par_1'}, use_global_device_ids=true, to_apply=%region_34.35 | all-reduce | flops 32 | bytes 256 | tf_op jit(solution)/shard_map/psum | solution.py:50
  813.0 35.4 %all_to_all.143 = bf16[32,2,1024]{2,1,0:T(2,128)(2,1)S(1)} all-to-all(bf16[32,2,1024]{2,1,0:T(2,128)(2,1)S(1)} %reshape.419), channel_id=1, replica_groups=mesh['parts'=2,'pix'=32,'par_0'=4,'par_1'=2] {'pix'}, dimensions={0} | all-to-all | bytes 262144 | tf_op jit(solution)/shard_map/all_to_all | solution.py:30
  891.2 20.4 %all-to-all-done.18 = f32[32,1,32]{2,1,0:T(1,128)S(1)} async-done(((f32[32,1,32]{2,1,0:T(1,128)}), f32[32,1,32]{2,1,0:T(1,128)S(1)}, u32[]{:S(2)}, u32[]{:S(2)}) %all-to-all-start.18) | async-done | bytes 4128 | tf_op jit(solution)/shard_map/all_to_all | solution.py:30
  929.0 29.9 %all-to-all-done.20 = f32[32,1,2048]{2,1,0:T(1,128)S(1)} async-done(((f32[32,1,2048]{2,1,0:T(1,128)}), f32[32,1,2048]{2,1,0:T(1,128)S(1)}, u32[]{:S(2)}, u32[]{:S(2)}) %all-to-all-start.20) | async-done | bytes 262176 | tf_op jit(solution)/shard_map/all_to_all | solution.py:45
  960.6 40.2 %psum.117 = f32[32]{0:T(128)S(1)} all-reduce(f32[32]{0:T(128)S(1)} %dynamic_update_slice.19), channel_id=1, replica_groups=mesh['parts'=2,'pix'=32,'par_0'=4,'par_1'=2] {'pix'}, use_global_device_ids=true, to_apply=%region_42.43 | all-reduce | flops 32 | bytes 256 | tf_op jit(solution)/shard_map/psum | solution.py:50
  1007.6 21.8 %psum.119 = f32[32]{0:T(128)S(1)} all-reduce(f32[32]{0:T(128)S(1)} %psum.118), channel_id=1, replica_groups=mesh['parts'=2,'pix'=32,'par_0'=4,'par_1'=2] {'par_1'}, use_global_device_ids=true, to_apply=%region_44.45 | all-reduce | flops 32 | bytes 256 | tf_op jit(solution)/shard_map/psum | solution.py:50
  1032.2 35.4 %all_to_all.144 = bf16[32,2,1024]{2,1,0:T(2,128)(2,1)S(1)} all-to-all(bf16[32,2,1024]{2,1,0:T(2,128)(2,1)S(1)} %reshape.421), channel_id=1, replica_groups=mesh['parts'=2,'pix'=32,'par_0'=4,'par_1'=2] {'pix'}, dimensions={0} | all-to-all | bytes 262144 | tf_op jit(solution)/shard_map/all_to_all | solution.py:30
  1110.2 20.4 %all-to-all-done.23 = f32[32,1,32]{2,1,0:T(1,128)S(1)} async-done(((f32[32,1,32]{2,1,0:T(1,128)}), f32[32,1,32]{2,1,0:T(1,128)S(1)}, u32[]{:S(2)}, u32[]{:S(2)}) %all-to-all-start.23) | async-done | bytes 4128 | tf_op jit(solution)/shard_map/all_to_all | solution.py:30
  1141.4 37.4 %all-to-all-done.25 = f32[32,1,2048]{2,1,0:T(1,128)S(1)} async-done(((f32[32,1,2048]{2,1,0:T(1,128)}), f32[32,1,2048]{2,1,0:T(1,128)S(1)}, u32[]{:S(2)}, u32[]{:S(2)}) %all-to-all-start.25) | async-done | bytes 262176 | tf_op jit(solution)/shard_map/all_to_all | solution.py:30
  (241 shorter events, 406.5 us)
Async XLA Ops:
  4.9 87.3 %all-to-all-start = ((f32[32,1,2048]{2,1,0:T(1,128)}), f32[32,1,2048]{2,1,0:T(1,128)S(1)}, u32[]{:S(2)}, u32[]{:S(2)}) async-start(f32[32,1,2048]{2,1,0:T(1,128)} %copy.19), calls=%async_computation | async-start | bytes 524288 | tf_op jit(solution)/shard_map/all_to_all | solution.py:45
  132.2 24.7 %all-to-all-start.2 = ((f32[8,32,1152]{2,1,0:T(8,128)}), f32[8,32,1152]{2,1,0:T(8,128)S(1)}, u32[]{:S(2)}, u32[]{:S(2)}) async-start(f32[8,32,1152]{2,1,0:T(8,128)} %broadcast_in_dim.81), calls=%async_computation.2 | async-start | bytes 2359296 | tf_op jit(solution)/shard_map/all_to_all | solution.py:30
  140.5 15.5 %collective-permute-start = (f32[32,1,128]{2,1,0:T(1,128)S(1)}, f32[32,1,128]{2,1,0:T(1,128)S(1)}, u32[]{:S(2)}, u32[]{:S(2)}) collective-permute-start(f32[32,1,128]{2,1,0:T(1,128)S(1)} %get-tuple-element.33), channel_id=1, source_target_pairs={{1,0},{2,1},{3,2},{4,3},{5,4},{6,5},{7,6},{9,8},{10,9},{11,10},{12... | collective-permute-start | bytes 49160 | tf_op jit(solution)/shard_map/ppermute | solution.py:23
  142.5 13.6 %collective-permute-start.1 = (f32[32,1,128]{2,1,0:T(1,128)S(1)}, f32[32,1,128]{2,1,0:T(1,128)S(1)}, u32[]{:S(2)}, u32[]{:S(2)}) collective-permute-start(f32[32,1,128]{2,1,0:T(1,128)S(1)} %get-tuple-element.32), channel_id=1, source_target_pairs={{0,1},{1,2},{2,3},{3,4},{4,5},{5,6},{6,7},{8,9},{9,10},{10,11},{11... | collective-permute-start | bytes 49160 | tf_op jit(solution)/shard_map/ppermute | solution.py:20
  166.9 74.4 %all-to-all-start.3 = ((f32[32,1,32]{2,1,0:T(1,128)}), f32[32,1,32]{2,1,0:T(1,128)S(1)}, u32[]{:S(2)}, u32[]{:S(2)}) async-start(f32[32,1,32]{2,1,0:T(1,128)} %broadcast_in_dim.82), calls=%async_computation.3 | async-start | bytes 32768 | tf_op jit(solution)/shard_map/all_to_all | solution.py:30
  245.7 59.3 %all-to-all-start.5 = ((f32[32,1,2048]{2,1,0:T(1,128)}), f32[32,1,2048]{2,1,0:T(1,128)S(1)}, u32[]{:S(2)}, u32[]{:S(2)}) async-start(f32[32,1,2048]{2,1,0:T(1,128)} %copy.22), calls=%async_computation.5 | async-start | bytes 524288 | tf_op jit(solution)/shard_map/all_to_all | solution.py:45
  415.3 22.7 %all-to-all-start.7 = ((f32[8,32,1152]{2,1,0:T(8,128)}), f32[8,32,1152]{2,1,0:T(8,128)S(1)}, u32[]{:S(2)}, u32[]{:S(2)}) async-start(f32[8,32,1152]{2,1,0:T(8,128)} %broadcast_in_dim.86), calls=%async_computation.7 | async-start | bytes 2359296 | tf_op jit(solution)/shard_map/all_to_all | solution.py:30
  421.4 15.5 %collective-permute-start.4 = (f32[32,1,128]{2,1,0:T(1,128)S(1)}, f32[32,1,128]{2,1,0:T(1,128)S(1)}, u32[]{:S(2)}, u32[]{:S(2)}) collective-permute-start(f32[32,1,128]{2,1,0:T(1,128)S(1)} %get-tuple-element.31), channel_id=1, source_target_pairs={{1,0},{2,1},{3,2},{4,3},{5,4},{6,5},{7,6},{9,8},{10,9},{11,10},{12... | collective-permute-start | bytes 49160 | tf_op jit(solution)/shard_map/ppermute | solution.py:23
  423.7 13.3 %collective-permute-start.5 = (f32[32,1,128]{2,1,0:T(1,128)S(1)}, f32[32,1,128]{2,1,0:T(1,128)S(1)}, u32[]{:S(2)}, u32[]{:S(2)}) collective-permute-start(f32[32,1,128]{2,1,0:T(1,128)S(1)} %get-tuple-element.30), channel_id=1, source_target_pairs={{0,1},{1,2},{2,3},{3,4},{4,5},{5,6},{6,7},{8,9},{9,10},{10,11},{11... | collective-permute-start | bytes 49160 | tf_op jit(solution)/shard_map/ppermute | solution.py:20
  448.0 25.2 %all-to-all-start.8 = ((f32[32,1,32]{2,1,0:T(1,128)}), f32[32,1,32]{2,1,0:T(1,128)S(1)}, u32[]{:S(2)}, u32[]{:S(2)}) async-start(f32[32,1,32]{2,1,0:T(1,128)} %broadcast_in_dim.87), calls=%async_computation.8 | async-start | bytes 32768 | tf_op jit(solution)/shard_map/all_to_all | solution.py:30
  477.5 42.9 %all-to-all-start.10 = ((f32[32,1,2048]{2,1,0:T(1,128)}), f32[32,1,2048]{2,1,0:T(1,128)S(1)}, u32[]{:S(2)}, u32[]{:S(2)}) async-start(f32[32,1,2048]{2,1,0:T(1,128)} %copy.25), calls=%async_computation.10 | async-start | bytes 524288 | tf_op jit(solution)/shard_map/all_to_all | solution.py:45
  634.5 22.7 %all-to-all-start.12 = ((f32[8,32,1152]{2,1,0:T(8,128)}), f32[8,32,1152]{2,1,0:T(8,128)S(1)}, u32[]{:S(2)}, u32[]{:S(2)}) async-start(f32[8,32,1152]{2,1,0:T(8,128)} %broadcast_in_dim.90), calls=%async_computation.12 | async-start | bytes 2359296 | tf_op jit(solution)/shard_map/all_to_all | solution.py:30
  640.7 15.5 %collective-permute-start.8 = (f32[32,1,128]{2,1,0:T(1,128)S(1)}, f32[32,1,128]{2,1,0:T(1,128)S(1)}, u32[]{:S(2)}, u32[]{:S(2)}) collective-permute-start(f32[32,1,128]{2,1,0:T(1,128)S(1)} %get-tuple-element.29), channel_id=1, source_target_pairs={{1,0},{2,1},{3,2},{4,3},{5,4},{6,5},{7,6},{9,8},{10,9},{11,10},{12... | collective-permute-start | bytes 49160 | tf_op jit(solution)/shard_map/ppermute | solution.py:23
  667.2 25.2 %all-to-all-start.13 = ((f32[32,1,32]{2,1,0:T(1,128)}), f32[32,1,32]{2,1,0:T(1,128)S(1)}, u32[]{:S(2)}, u32[]{:S(2)}) async-start(f32[32,1,32]{2,1,0:T(1,128)} %broadcast_in_dim.91), calls=%async_computation.13 | async-start | bytes 32768 | tf_op jit(solution)/shard_map/all_to_all | solution.py:30
  696.7 42.9 %all-to-all-start.15 = ((f32[32,1,2048]{2,1,0:T(1,128)}), f32[32,1,2048]{2,1,0:T(1,128)S(1)}, u32[]{:S(2)}, u32[]{:S(2)}) async-start(f32[32,1,2048]{2,1,0:T(1,128)} %copy.28), calls=%async_computation.15 | async-start | bytes 524288 | tf_op jit(solution)/shard_map/all_to_all | solution.py:45
  853.5 22.7 %all-to-all-start.17 = ((f32[8,32,1152]{2,1,0:T(8,128)}), f32[8,32,1152]{2,1,0:T(8,128)S(1)}, u32[]{:S(2)}, u32[]{:S(2)}) async-start(f32[8,32,1152]{2,1,0:T(8,128)} %broadcast_in_dim.94), calls=%async_computation.17 | async-start | bytes 2359296 | tf_op jit(solution)/shard_map/all_to_all | solution.py:30
  859.7 15.5 %collective-permute-start.12 = (f32[32,1,128]{2,1,0:T(1,128)S(1)}, f32[32,1,128]{2,1,0:T(1,128)S(1)}, u32[]{:S(2)}, u32[]{:S(2)}) collective-permute-start(f32[32,1,128]{2,1,0:T(1,128)S(1)} %get-tuple-element.27), channel_id=1, source_target_pairs={{1,0},{2,1},{3,2},{4,3},{5,4},{6,5},{7,6},{9,8},{10,9},{11,10},{12... | collective-permute-start | bytes 49160 | tf_op jit(solution)/shard_map/ppermute | solution.py:23
  886.2 25.5 %all-to-all-start.18 = ((f32[32,1,32]{2,1,0:T(1,128)}), f32[32,1,32]{2,1,0:T(1,128)S(1)}, u32[]{:S(2)}, u32[]{:S(2)}) async-start(f32[32,1,32]{2,1,0:T(1,128)} %broadcast_in_dim.95), calls=%async_computation.18 | async-start | bytes 32768 | tf_op jit(solution)/shard_map/all_to_all | solution.py:30
  916.0 42.9 %all-to-all-start.20 = ((f32[32,1,2048]{2,1,0:T(1,128)}), f32[32,1,2048]{2,1,0:T(1,128)S(1)}, u32[]{:S(2)}, u32[]{:S(2)}) async-start(f32[32,1,2048]{2,1,0:T(1,128)} %copy.31), calls=%async_computation.20 | async-start | bytes 524288 | tf_op jit(solution)/shard_map/all_to_all | solution.py:45
  1072.8 22.7 %all-to-all-start.22 = ((f32[8,32,1152]{2,1,0:T(8,128)}), f32[8,32,1152]{2,1,0:T(8,128)S(1)}, u32[]{:S(2)}, u32[]{:S(2)}) async-start(f32[8,32,1152]{2,1,0:T(8,128)} %broadcast_in_dim.98), calls=%async_computation.22 | async-start | bytes 2359296 | tf_op jit(solution)/shard_map/all_to_all | solution.py:30
  1079.0 15.5 %collective-permute-start.16 = (f32[32,1,128]{2,1,0:T(1,128)S(1)}, f32[32,1,128]{2,1,0:T(1,128)S(1)}, u32[]{:S(2)}, u32[]{:S(2)}) collective-permute-start(f32[32,1,128]{2,1,0:T(1,128)S(1)} %get-tuple-element.25), channel_id=1, source_target_pairs={{1,0},{2,1},{3,2},{4,3},{5,4},{6,5},{7,6},{9,8},{10,9},{11,10},{12... | collective-permute-start | bytes 49160 | tf_op jit(solution)/shard_map/ppermute | solution.py:23
  1081.2 13.3 %collective-permute-start.17 = (f32[32,1,128]{2,1,0:T(1,128)S(1)}, f32[32,1,128]{2,1,0:T(1,128)S(1)}, u32[]{:S(2)}, u32[]{:S(2)}) collective-permute-start(f32[32,1,128]{2,1,0:T(1,128)S(1)} %get-tuple-element.24), channel_id=1, source_target_pairs={{0,1},{1,2},{2,3},{3,4},{4,5},{5,6},{6,7},{8,9},{9,10},{10,11},{11... | collective-permute-start | bytes 49160 | tf_op jit(solution)/shard_map/ppermute | solution.py:20
  1105.5 25.2 %all-to-all-start.23 = ((f32[32,1,32]{2,1,0:T(1,128)}), f32[32,1,32]{2,1,0:T(1,128)S(1)}, u32[]{:S(2)}, u32[]{:S(2)}) async-start(f32[32,1,32]{2,1,0:T(1,128)} %broadcast_in_dim.99), calls=%async_computation.23 | async-start | bytes 32768 | tf_op jit(solution)/shard_map/all_to_all | solution.py:30
  1135.9 42.9 %all-to-all-start.25 = ((f32[32,1,2048]{2,1,0:T(1,128)}), f32[32,1,2048]{2,1,0:T(1,128)S(1)}, u32[]{:S(2)}, u32[]{:S(2)}) async-start(f32[32,1,2048]{2,1,0:T(1,128)} %broadcast_in_dim.101), calls=%async_computation.25 | async-start | bytes 524288 | tf_op jit(solution)/shard_map/all_to_all | solution.py:30
  (16 other events, 217.1 us)
where the time goes:
time: 1190 us; the launch traced here: 1180 us
  blocking collectives  515 us (43%)
  waiting for transfers between devices  358 us (30%)
  starting transfers between devices  212 us (18%)
  matrix products  35.5 us (3%)
  local copies, waits for them, and re-layouts  30.7 us (3%)
  other arithmetic  27.6 us (2%)
    psum x15, blocking collectives, by_axis(): return functools.reduce(lax.psum, axes, shard)  341 us
    all_to_all x5, blocking collectives, sent_to_all(): return lax.all_to_all(copies, axis, split_axis=0, concat_axis=0, tiled=True)  174 us
    all_to_all x5, waiting for transfers between devices, sum_at_owner(): lax.all_to_all(cut_along(shard, dim, length), axis, 0, 0, tiled=True)  164 us
    all_to_all x16, waiting for transfers between devices, sent_to_all(): return lax.all_to_all(copies, axis, split_axis=0, concat_axis=0, tiled=True)  141 us
    all_to_all x16, starting transfers between devices, sent_to_all(): return lax.all_to_all(copies, axis, split_axis=0, concat_axis=0, tiled=True)  82.1 us
    all_to_all x5, starting transfers between devices, sum_at_owner(): lax.all_to_all(cut_along(shard, dim, length), axis, 0, 0, tiled=True)  78.6 us
    ppermute x9, waiting for transfers between devices, padded_2(): lax.ppermute(lax.slice_in_dim(block, 0, width, axis=dim), axis, backward)  49.5 us
    ppermute x9, starting transfers between devices, padded_2(): lax.ppermute(lax.slice_in_dim(block, block.shape[dim] - width, None, axis...  26.7 us
  transfers between devices with their start and end apart: 39, of which 24 were waited for; matrix products, arithmetic and copies ran while one was open for 1% of the time, Pallas kernels for 0%

commit v1 on v0

v1 whole, which is shorter than its diff:
```python
import functools

import jax
import jax.numpy as jnp
from jax import lax
from jax.experimental import pallas as pl
from jax.experimental.pallas import tpu as pltpu
from jax.sharding import PartitionSpec as P

GRID = 128
ITERS = 5
WINDOW = 8
NEAR = (4, -3, 3, -2, 2, -1, 1)
F32 = jnp.float32
BF16 = jnp.bfloat16
MESH = pl.DeviceIdType.MESH


def row_sums(value, eye):
    column = jnp.sum(value, axis=1, keepdims=True)
    return jnp.sum(jnp.where(eye, column, 0.0), axis=0, keepdims=True)


def to_column(row, eye):
    return jnp.sum(jnp.where(eye, row, 0.0), axis=1, keepdims=True)


def kernel(
    n_pix, n_par, green, observed, sol_out, res_out,
    gmat, grad, near_send, near_recv, near_low, near_low_recv, own_part, wide_send, wide_recv,
    wide_low, wide_low_recv, rows_near, rows_wide,
    near_grad, halo, direction, smooth1, smooth2, solution, residual, image, image_bf,
    partial, pair_recv, chip_buf, half_send, half_recv, fresh_rows, smooth_rows, final_rows, row_send,
    g_sem, as_sem, ar_sem, bs_sem, br_sem, cs_sem, cr_sem, hs_sem, hr_sem, xs_sem, x1r_sem, x2r_sem,
    x3r_sem, fs_sem, fr_sem, ss_sem, sr_sem, zs_sem, zr_sem, ars_sem, arr_sem, brs_sem, brr_sem,
    als_sem, alr_sem, bls_sem, blr_sem,
):
    sets = observed.shape[0]
    pixels = observed.shape[1]
    chunk = gmat.shape[2]
    rows_per = chunk // GRID
    blocks = n_pix // WINDOW
    rows = direction.shape[0] - 2 * rows_per
    half = sets // 2
    z = lax.axis_index("pix")
    par = lax.axis_index("par")
    core = lax.rem(par, 2)
    chip = lax.div(par, 2)
    chips = n_par // 2
    mate = par + 1 - 2 * core
    own_class = lax.rem(z, WINDOW)
    own_block = lax.div(z, WINDOW)

    def at_pix(offset):
        return {"pix": lax.rem(z + (offset + n_pix), n_pix)}

    def at_par(offset):
        return {"par": lax.rem(par + offset, n_par)}

    def class_at(offset):
        return lax.rem(z + (offset + n_pix), WINDOW)

    def remote(src, dst, send, recv, device):
        return pltpu.make_async_remote_copy(
            src_ref=src, dst_ref=dst, send_sem=send, recv_sem=recv, device_id=device, device_id_type=MESH
        )

    loads = []
    for index in range(WINDOW):
        load = pltpu.make_async_copy(
            green.at[:, pl.ds(index * chunk, chunk)], gmat.at[index], g_sem.at[index]
        )
        load.start()
        loads.append(load)

    halo[...] = jnp.zeros_like(halo)
    smooth_rows[...] = jnp.zeros_like(smooth_rows)
    barrier = pltpu.get_barrier_semaphore()
    for offset in range(1, n_pix):
        pl.semaphore_signal(barrier, inc=1, device_id=at_pix(offset), device_id_type=MESH)
    for offset in range(1, n_par):
        pl.semaphore_signal(barrier, inc=1, device_id=at_par(offset), device_id_type=MESH)

    lane = lax.broadcasted_iota(jnp.int32, (sets, GRID), 1)
    eye = lane == lax.broadcasted_iota(jnp.int32, (sets, GRID), 0)
    first_lane = lane == 0
    last_lane = lane == GRID - 1

    direction[...] = jnp.zeros_like(direction)
    smooth2[...] = jnp.zeros_like(smooth2)
    smooth1[...] = jnp.zeros_like(smooth1)
    solution[...] = jnp.zeros_like(solution)
    image[...] = jnp.zeros_like(image)
    grad[...] = jnp.zeros_like(grad)
    image_bf[...] = observed[...]
    residual[...] = observed[...].astype(F32)
    for load in loads:
        load.wait()
    pl.semaphore_wait(barrier, n_pix - 1 + n_par - 1)

    def all_par(rows_ref, row, slot_sem, send_sem, index):
        row_send[index] = row
        rows_ref[par] = row
        for offset in range(1, n_par):
            remote(
                row_send.at[index], rows_ref.at[par], send_sem, slot_sem, at_par(offset)
            ).start()

    def wait_rows(rows_ref, sem, count):
        part = rows_ref.at[pl.ds(0, count)]
        remote(part, part, sem, sem, at_par(1)).wait_recv()

    def neighbours_sum(field, row):
        here = field[row]
        left = jnp.where(first_lane, 0.0, pltpu.roll(here, 1, 1))
        right = jnp.where(last_lane, 0.0, pltpu.roll(here, GRID - 1, 1))
        return here, left + right

    def sum_par(rows_ref):
        total = rows_ref[0]
        for index in range(1, n_par):
            total = total + rows_ref[index]
        return total

    def sweep_body(sweep, grad_sq):
        parity = lax.rem(sweep, 2)
        started = sweep > 0

        lhs = image_bf[...]
        for slot, offset in enumerate(NEAR):
            product = jnp.dot(lhs, gmat[class_at(offset)], preferred_element_type=F32)
            rounded = product.astype(BF16)
            near_send[slot] = rounded
            remote(near_send.at[slot], near_recv.at[slot], as_sem, ar_sem, at_pix(offset)).start()

            @pl.when(jnp.logical_not(started))
            def _():
                near_low[slot] = (product - rounded.astype(F32)).astype(BF16)
                remote(
                    near_low.at[slot], near_low_recv.at[slot], als_sem, alr_sem, at_pix(offset)
                ).start()

        value = image[...]
        image_row = row_sums(value * value, eye)
        row_send[2] = image_row
        rows_near[len(NEAR)] = image_row
        for slot, offset in enumerate(NEAR):
            remote(row_send.at[2], rows_near.at[slot], ars_sem, arr_sem, at_pix(offset)).start()
        total = jnp.dot(lhs, gmat[own_class], preferred_element_type=F32)
        remote(near_recv, near_recv, ar_sem, ar_sem, at_pix(1)).wait_recv()
        for slot in range(len(NEAR)):
            total = total + near_recv[slot].astype(F32)
        own_part[...] = total

        @pl.when(jnp.logical_not(started))
        def _():
            remote(near_low_recv, near_low_recv, als_sem, alr_sem, at_pix(1)).wait_recv()
            more = near_low_recv[0].astype(F32)
            for slot in range(1, len(NEAR)):
                more = more + near_low_recv[slot].astype(F32)
            own_part[...] += more

        total = own_part[...]
        rounded = total.astype(BF16)
        wide_send[...] = rounded
        wide_recv[parity, 0] = rounded
        order = [blocks // 2] + [b for b in range(1, blocks) if b != blocks // 2]
        for block in order:
            remote(
                wide_send, wide_recv.at[parity, blocks - block], bs_sem, br_sem.at[parity],
                at_pix(block * WINDOW),
            ).start()

        @pl.when(jnp.logical_not(started))
        def _():
            low_part = (total - rounded.astype(F32)).astype(BF16)
            wide_low[...] = low_part
            wide_low_recv[0] = low_part
            for block in order:
                remote(
                    wide_low, wide_low_recv.at[blocks - block], bls_sem, blr_sem,
                    at_pix(block * WINDOW),
                ).start()

        part = rows_near.at[pl.ds(0, len(NEAR))]
        remote(part, part, arr_sem, arr_sem, at_pix(1)).wait_recv()
        for slot in range(WINDOW):
            rows_wide[parity, 0, slot] = rows_near[slot]
        for block in order:
            remote(
                rows_wide.at[parity, 0], rows_wide.at[parity, blocks - block], brs_sem, brr_sem.at[parity],
                at_pix(block * WINDOW),
            ).start()

        @pl.when(started)
        def _():
            wait_rows(smooth_rows, sr_sem, n_par - 1)

        smooth_sq = sum_par(smooth_rows)

        part = rows_wide.at[parity, pl.ds(0, blocks - 1)]
        remote(part, part, brs_sem, brr_sem.at[parity], at_pix(1)).wait_recv()
        image_sq = canonical_rows(parity)
        step_row = jnp.where(started, grad_sq / (image_sq + smooth_sq), -1.0)
        step = to_column(step_row, eye)

        part = wide_recv.at[parity, pl.ds(0, blocks - 1)]
        remote(part, part, bs_sem, br_sem.at[parity], at_pix(1)).wait_recv()
        total = None
        for block in range(blocks):
            term = wide_recv[parity, lax.rem(block - own_block + blocks, blocks)].astype(F32)
            total = term if total is None else total + term
        own_part[...] = total

        @pl.when(jnp.logical_not(started))
        def _():
            part = wide_low_recv.at[pl.ds(0, blocks - 1)]
            remote(part, part, bls_sem, blr_sem, at_pix(1)).wait_recv()
            more = None
            for block in range(blocks):
                place = lax.rem(block - own_block + blocks, blocks)
                term = wide_low_recv[place].astype(F32)
                more = term if more is None else more + term
            own_part[...] += more
            remote(near_low, near_low, als_sem, alr_sem, at_pix(1)).wait_send()
            remote(part, part, bls_sem, blr_sem, at_pix(1)).wait_send()

        total = own_part[...]
        for index in range(rows_per):
            cut = slice(index * GRID, (index + 1) * GRID)
            full = total[:, cut] + smooth2[own_class * rows_per + index]
            grad[:, cut] = grad[:, cut] - step * full
        rounded = grad[...].astype(BF16)
        near_grad[own_class] = rounded
        for offset in NEAR:
            remote(
                near_grad.at[own_class], near_grad.at[own_class], cs_sem, cr_sem.at[offset + 3],
                at_pix(-offset),
            ).start()

        residual[...] = residual[...] - step * image[...]

        def taken(index):
            block = near_grad[index]
            value = block.astype(F32)
            return (
                lax.dot_general(
                    block, gmat[index], (((1,), (1,)), ((), ())), preferred_element_type=F32
                ),
                value * value,
            )

        product, squares = taken(own_class)
        partial[...] = product
        for offset in (1, -1, 2, -2, 3, -3, 4):
            remote(
                near_grad.at[0], near_grad.at[0], cs_sem, cr_sem.at[offset + 3], at_pix(1)
            ).wait_recv()
            product, more = taken(class_at(offset))
            partial[...] += product
            squares = squares + more
        all_par(fresh_rows, row_sums(squares, eye), fr_sem, fs_sem, 0)
        away = remote(
            partial.at[pl.ds(pl.multiple_of((1 - core) * half, half), half)], pair_recv,
            xs_sem.at[0], x1r_sem, {"par": mate},
        )
        away.start()

        low = remote(near_grad.at[0], halo.at[1], hs_sem.at[0], hr_sem.at[1], {"par": lax.rem(par + n_par - 1, n_par)})
        high = remote(near_grad.at[WINDOW - 1], halo.at[0], hs_sem.at[1], hr_sem.at[0], at_par(1))

        @pl.when(par > 0)
        def _():
            low.start()

        @pl.when(par < n_par - 1)
        def _():
            high.start()

        away.wait_recv()
        mine = partial[pl.ds(pl.multiple_of(core * half, half), half)] + pair_recv[...]
        chip_buf[parity, chip] = mine.astype(BF16)
        for offset in (2, 1, 3):
            remote(
                chip_buf.at[parity, chip], chip_buf.at[parity, chip], xs_sem.at[1], x2r_sem.at[parity],
                at_par(2 * offset),
            ).start()

        wait_rows(fresh_rows, fr_sem, n_par - 1)
        fresh_sq = sum_par(fresh_rows)
        ratio_row = jnp.where(started, fresh_sq / grad_sq, 0.0)
        ratio = to_column(ratio_row, eye)
        for row in range(rows):
            old = direction[row + rows_per]
            solution[row] = solution[row] + step * old
            cut = slice(row % rows_per * GRID, (row % rows_per + 1) * GRID)
            new = near_grad[row // rows_per, :, cut].astype(F32)
            direction[row + rows_per] = new + ratio * old

        @pl.when(par < n_par - 1)
        def _():
            low.wait_recv()

        @pl.when(par > 0)
        def _():
            high.wait_recv()

        for index in range(rows_per):
            cut = slice(index * GRID, (index + 1) * GRID)
            direction[index] = halo[0, :, cut].astype(F32) + ratio * direction[index]
            top = rows + rows_per + index
            direction[top] = halo[1, :, cut].astype(F32) + ratio * direction[top]

        squares = None
        for row in range(rows + 2):
            here, beside = neighbours_sum(direction, row + rows_per - 1)
            beside = beside + direction[row + rows_per - 2] + direction[row + rows_per]
            value = here - 0.25 * beside
            if row == 0:
                value = jnp.where(par > 0, value, 0.0)
            elif row == rows + 1:
                value = jnp.where(par < n_par - 1, value, 0.0)
            else:
                squares = value * value if squares is None else squares + value * value
            smooth1[row] = value
        all_par(smooth_rows, row_sums(squares, eye), sr_sem, ss_sem, 1)
        for row in range(rows):
            here, beside = neighbours_sum(smooth1, row + 1)
            smooth2[row] = here - 0.25 * (beside + smooth1[row] + smooth1[row + 2])

        part = chip_buf.at[parity, pl.ds(0, chips - 1)]
        remote(part, part, xs_sem.at[1], x2r_sem.at[parity], at_par(1)).wait_recv()
        total = chip_buf[parity, 0].astype(F32)
        for index in range(1, chips):
            total = total + chip_buf[parity, index].astype(F32)
        my_rows = pl.ds(pl.multiple_of(core * half, half), half)
        their_rows = pl.ds(pl.multiple_of((1 - core) * half, half), half)
        half_send[...] = total
        back = remote(half_send, half_recv, xs_sem.at[2], x3r_sem, {"par": mate})
        back.start()
        partial[my_rows] = total
        away.wait_send()
        back.wait_recv()
        partial[their_rows] = half_recv[...]
        value = partial[...] + ratio * image[...]
        image[...] = value
        image_bf[...] = value.astype(BF16)

        remote(near_send, near_send, as_sem, as_sem, at_pix(1)).wait_send()
        part = rows_near.at[pl.ds(0, len(NEAR))]
        remote(part, part, ars_sem, ars_sem, at_pix(1)).wait_send()
        part = wide_recv.at[parity, pl.ds(0, blocks - 1)]
        remote(part, part, bs_sem, bs_sem, at_pix(1)).wait_send()
        part = rows_wide.at[parity, pl.ds(0, blocks - 1)]
        remote(part, part, brs_sem, brs_sem, at_pix(1)).wait_send()
        remote(near_send, near_send, cs_sem, cs_sem, at_pix(1)).wait_send()
        part = fresh_rows.at[pl.ds(0, n_par - 1)]
        remote(part, part, fs_sem, fs_sem, at_pix(1)).wait_send()
        remote(part, part, ss_sem, ss_sem, at_pix(1)).wait_send()
        part = chip_buf.at[parity, pl.ds(0, chips - 1)]
        remote(part, part, xs_sem.at[1], xs_sem.at[1], at_par(1)).wait_send()
        back.wait_send()

        @pl.when(par > 0)
        def _():
            low.wait_send()

        @pl.when(par < n_par - 1)
        def _():
            high.wait_send()

        return fresh_sq

    def canonical_rows(parity):
        total = None
        for shard in range(n_pix):
            back = lax.rem(shard - z + (2 * n_pix + WINDOW // 2), n_pix)
            block = lax.div(back, WINDOW)
            inside = lax.rem(back, WINDOW)
            row = rows_wide[parity, block, slot_of(inside)]
            total = row if total is None else total + row
        return total

    def slot_of(inside):
        offset = WINDOW // 2 - inside
        slot = len(NEAR)
        for index, value in enumerate(NEAR):
            slot = jnp.where(offset == value, index, slot)
        return slot

    grad_sq = lax.fori_loop(0, ITERS, sweep_body, jnp.zeros((1, GRID), F32))

    value = image[...]
    image_row = row_sums(value * value, eye)
    row_send[2] = image_row
    final_rows[z] = image_row
    for offset in [s * d for d in range(n_pix // 2, 0, -1) for s in (1, -1)][1:]:
        remote(row_send.at[2], final_rows.at[z], zs_sem, zr_sem, at_pix(offset)).start()
    wait_rows(smooth_rows, sr_sem, n_par - 1)
    smooth_sq = sum_par(smooth_rows)
    part = final_rows.at[pl.ds(0, n_pix - 1)]
    remote(part, part, zs_sem, zr_sem, at_pix(1)).wait_recv()
    image_sq = final_rows[0]
    for shard in range(1, n_pix):
        image_sq = image_sq + final_rows[shard]
    step = to_column(grad_sq / (image_sq + smooth_sq), eye)
    for row in range(rows):
        sol_out[:, row * GRID : (row + 1) * GRID] = solution[row] + step * direction[row + rows_per]
    res_out[...] = residual[...] - step * image[...]
    remote(part, part, zs_sem, zs_sem, at_pix(1)).wait_send()


def solution(mesh):
    n_pix, n_par = mesh.shape["pix"], mesh.shape["par"]

    def on_device(green_matrix, observed):
        pixels, cells = green_matrix.shape
        sets = observed.shape[0]
        chunk = cells // WINDOW
        rows = cells // GRID
        extra = chunk // GRID
        blocks = n_pix // WINDOW
        half = sets // 2
        near = len(NEAR)
        dma = pltpu.SemaphoreType.DMA
        vmem = pltpu.VMEM
        return pl.pallas_call(
            functools.partial(kernel, n_pix, n_par),
            out_shape=(
                jax.ShapeDtypeStruct((sets, cells), F32),
                jax.ShapeDtypeStruct((sets, pixels), F32),
            ),
            in_specs=[
                pl.BlockSpec(memory_space=pl.ANY),
                pl.BlockSpec(memory_space=pltpu.VMEM),
            ],
            out_specs=(
                pl.BlockSpec(memory_space=pltpu.VMEM),
                pl.BlockSpec(memory_space=pltpu.VMEM),
            ),
            scratch_shapes=[
                vmem((WINDOW, pixels, chunk), BF16),
                vmem((sets, chunk), F32),
                vmem((near, sets, chunk), BF16),
                vmem((near, sets, chunk), BF16),
                vmem((near, sets, chunk), BF16),
                vmem((near, sets, chunk), BF16),
                vmem((sets, chunk), F32),
                vmem((sets, chunk), BF16),
                vmem((2, blocks, sets, chunk), BF16),
                vmem((sets, chunk), BF16),
                vmem((blocks, sets, chunk), BF16),
                vmem((WINDOW, 1, GRID), F32),
                vmem((2, blocks, WINDOW, 1, GRID), F32),
                vmem((WINDOW, sets, chunk), BF16),
                vmem((2, sets, chunk), BF16),
                vmem((rows + 2 * extra, sets, GRID), F32),
                vmem((rows + 2, sets, GRID), F32),
                vmem((rows, sets, GRID), F32),
                vmem((rows, sets, GRID), F32),
                vmem((sets, pixels), F32),
                vmem((sets, pixels), F32),
                vmem((sets, pixels), BF16),
                vmem((sets, pixels), F32),
                vmem((half, pixels), F32),
                vmem((2, n_par // 2, half, pixels), BF16),
                vmem((half, pixels), F32),
                vmem((half, pixels), F32),
                vmem((n_par, 1, GRID), F32),
                vmem((n_par, 1, GRID), F32),
                vmem((n_pix, 1, GRID), F32),
                vmem((3, 1, GRID), F32),
                dma((WINDOW,)),
                dma, dma,
                dma, dma((2,)),
                dma, dma((WINDOW,)),
                dma((2,)), dma((2,)),
                dma((3,)), dma, dma((2,)), dma,
                dma, dma,
                dma, dma,
                dma, dma,
                dma, dma,
                dma, dma((2,)),
                dma, dma, dma, dma,
            ],
            compiler_params=pltpu.CompilerParams(collective_id=0, has_side_effects=True),
        )(green_matrix, observed)

    return jax.shard_map(
        on_device,
        mesh=mesh,
        in_specs=(P("pix", "par"), P("parts", "pix")),
        out_specs=(P("parts", "par"), P("parts", "pix")),
        check_vma=False,
    )
```

time: 1190 us -> 253 us (0.21)
  blocking collectives: 515 us -> 0 us
  waiting for transfers between devices: 358 us -> 0 us
  Pallas kernels: 0 us -> 249 us
  starting transfers between devices: 212 us -> 0 us
  matrix products: 35.5 us -> 0 us
  other arithmetic: 27.6 us -> 0 us
  local copies, waits for them, and re-layouts: 30.7 us -> 3.25 us
    psum x15 -> x0, blocking collectives: 341 us -> none  [by_axis(): return functools.reduce(lax.psum, axes, shard)]
    all_to_all x21 -> x0, waiting for transfers between devices: 305 us -> none  [the longest x5 164 us: sum_at_owner(): lax.all_to_all(cut_along(shard, dim, length), axis, 0, 0, tiled=True)]
    pallas_call x0 -> x1, Pallas kernels: none -> 249 us  [on_device(): pl.pallas_call(functools.partial(kernel, n_pix, n_par), out_shape=(jax.Sh...]
    all_to_all x5 -> x0, blocking collectives: 174 us -> none  [sent_to_all(): return lax.all_to_all(copies, axis, split_axis=0, concat_axis=0, tiled=True)]
    all_to_all x21 -> x0, starting transfers between devices: 161 us -> none  [the longest x16 82.1 us: sent_to_all(): return lax.all_to_all(copies, axis, split_axis=0, concat_axis=0, tiled=True)]
    ppermute x18 -> x0, waiting for transfers between devices: 52.9 us -> none  [the longest x9 49.5 us: padded_2(): lax.ppermute(lax.slice_in_dim(block, 0, width, axis=dim), axis, backward)]
    ppermute x18 -> x0, starting transfers between devices: 51.5 us -> none  [the longest x9 26.7 us: padded_2(): lax.ppermute(lax.slice_in_dim(block, block.shape[dim] - width, None, axis...]
    dot_general x10 -> x0, matrix products: 35.5 us -> none  [the longest x5 19.1 us: forward(): lax.dot_general(rounded, green_matrix, (((1,), (1,)), ((), ())), preferre...]
  transfers between devices with their start and end apart: 39 -> 0, of which waited for: 24 -> 0; matrix products, arithmetic and copies ran while one was open for 1% -> 0% of each run, Pallas kernels for 0% -> 0%
where the time goes in v1:
time: 253 us
  Pallas kernels  249 us (98%)
  local copies, waits for them, and re-layouts  3.25 us (1%)
    pallas_call x1, Pallas kernels, on_device(): pl.pallas_call(functools.partial(kernel, n_pix, n_par), out_shape=(jax.Sh...  249 us

profile of v1, /device:TPU:33, one launch (start us, length us, event | category | flops | bytes accessed | tf_op | source)
XLA Modules:
  0.0 252.5 jit_solution(2268876903273811665)
XLA Ops:
  0.6 248.6 %shard_map.41 = (f32[32,2048]{1,0:T(8,128)}, f32[32,1152]{1,0:T(8,128)}) custom-call(bf16[1152,2048]{1,0:T(8,128)(2,1)} %green.1, bf16[32,1152]{1,0:T(8,128)(2,1)} %observed.1), custom_call_target="tpu_custom_call" | custom-call | tf_op jit(solution)/shard_map/pallas_call | solution.py:427
  249.3 1.7 copy.6
  251.0 1.6 copy.7

commit v2 on v1

--- a/solution.py
+++ b/solution.py
@@ -31,6 +31,7 @@
     wide_low, wide_low_recv, rows_near, rows_wide,
     near_grad, halo, direction, smooth1, smooth2, solution, residual, image, image_bf,
     partial, pair_recv, chip_buf, half_send, half_recv, fresh_rows, smooth_rows, final_rows, row_send,
+    ratio_buf,
     g_sem, as_sem, ar_sem, bs_sem, br_sem, cs_sem, cr_sem, hs_sem, hr_sem, xs_sem, x1r_sem, x2r_sem,
     x3r_sem, fs_sem, fr_sem, ss_sem, sr_sem, zs_sem, zr_sem, ars_sem, arr_sem, brs_sem, brr_sem,
     als_sem, alr_sem, bls_sem, blr_sem,
@@ -50,6 +51,10 @@
     mate = par + 1 - 2 * core
     own_class = lax.rem(z, WINDOW)
     own_block = lax.div(z, WINDOW)
+    early = jnp.where(z < n_pix // 2, 1, blocks - 1)
+    tiles = pixels // GRID
+    edge = (tiles + 1) // 2 * GRID
+    parts = ((0, edge), (edge, pixels - edge))
 
     def at_pix(offset):
         return {"pix": lax.rem(z + (offset + n_pix), n_pix)}
@@ -65,19 +70,20 @@
             src_ref=src, dst_ref=dst, send_sem=send, recv_sem=recv, device_id=device, device_id_type=MESH
         )
 
-    loads = []
-    for index in range(WINDOW):
-        load = pltpu.make_async_copy(
-            green.at[:, pl.ds(index * chunk, chunk)], gmat.at[index], g_sem.at[index]
-        )
-        load.start()
-        loads.append(load)
+    def matrix_load(index, offset):
+        place = class_at(offset)
+        columns = pl.ds(pl.multiple_of(place * chunk, chunk), chunk)
+        return pltpu.make_async_copy(green.at[:, columns], gmat.at[place], g_sem.at[index])
+
+    for index, offset in enumerate(NEAR + (0,)):
+        matrix_load(index, offset).start()
 
     halo[...] = jnp.zeros_like(halo)
     smooth_rows[...] = jnp.zeros_like(smooth_rows)
     barrier = pltpu.get_barrier_semaphore()
-    for offset in range(1, n_pix):
-        pl.semaphore_signal(barrier, inc=1, device_id=at_pix(offset), device_id_type=MESH)
+    for offset in range(1, WINDOW // 2 + 1):
+        for place in (offset, -offset):
+            pl.semaphore_signal(barrier, inc=1, device_id=at_pix(place), device_id_type=MESH)
     for offset in range(1, n_par):
         pl.semaphore_signal(barrier, inc=1, device_id=at_par(offset), device_id_type=MESH)
 
@@ -94,9 +100,7 @@
     grad[...] = jnp.zeros_like(grad)
     image_bf[...] = observed[...]
     residual[...] = observed[...].astype(F32)
-    for load in loads:
-        load.wait()
-    pl.semaphore_wait(barrier, n_pix - 1 + n_par - 1)
+    pl.semaphore_wait(barrier, WINDOW + n_par - 1)
 
     def all_par(rows_ref, row, slot_sem, send_sem, index):
         row_send[index] = row
@@ -122,37 +126,59 @@
             total = total + rows_ref[index]
         return total
 
+    def send_near(source, target, slot, offset, send, recv):
+        if offset == WINDOW // 2:
+            for part, place in enumerate((offset, -offset)):
+                cut = pl.ds(part * half, half)
+                remote(
+                    source.at[slot, cut], target.at[slot, cut], send, recv, at_pix(place)
+                ).start()
+        else:
+            remote(source.at[slot], target.at[slot], send, recv, at_pix(offset)).start()
+
     def sweep_body(sweep, grad_sq):
         parity = lax.rem(sweep, 2)
         started = sweep > 0
+        first = sweep == 0
 
         lhs = image_bf[...]
         for slot, offset in enumerate(NEAR):
+
+            @pl.when(first)
+            def _():
+                matrix_load(slot, offset).wait()
+
             product = jnp.dot(lhs, gmat[class_at(offset)], preferred_element_type=F32)
             rounded = product.astype(BF16)
             near_send[slot] = rounded
-            remote(near_send.at[slot], near_recv.at[slot], as_sem, ar_sem, at_pix(offset)).start()
-
-            @pl.when(jnp.logical_not(started))
+            send_near(near_send, near_recv, slot, offset, as_sem, ar_sem)
+
+            @pl.when(first)
             def _():
                 near_low[slot] = (product - rounded.astype(F32)).astype(BF16)
-                remote(
-                    near_low.at[slot], near_low_recv.at[slot], als_sem, alr_sem, at_pix(offset)
-                ).start()
-
-        value = image[...]
-        image_row = row_sums(value * value, eye)
-        row_send[2] = image_row
-        rows_near[len(NEAR)] = image_row
-        for slot, offset in enumerate(NEAR):
-            remote(row_send.at[2], rows_near.at[slot], ars_sem, arr_sem, at_pix(offset)).start()
+                send_near(near_low, near_low_recv, slot, offset, als_sem, alr_sem)
+
+            if slot == 1:
+                value = image[...]
+                image_row = row_sums(value * value, eye)
+                row_send[2] = image_row
+                rows_near[len(NEAR)] = image_row
+                for place, target in enumerate(NEAR):
+                    remote(
+                        row_send.at[2], rows_near.at[place], ars_sem, arr_sem, at_pix(target)
+                    ).start()
+
+        @pl.when(first)
+        def _():
+            matrix_load(len(NEAR), 0).wait()
+
         total = jnp.dot(lhs, gmat[own_class], preferred_element_type=F32)
         remote(near_recv, near_recv, ar_sem, ar_sem, at_pix(1)).wait_recv()
         for slot in range(len(NEAR)):
             total = total + near_recv[slot].astype(F32)
         own_part[...] = total
 
-        @pl.when(jnp.logical_not(started))
+        @pl.when(first)
         def _():
             remote(near_low_recv, near_low_recv, als_sem, alr_sem, at_pix(1)).wait_recv()
             more = near_low_recv[0].astype(F32)
@@ -164,33 +190,53 @@
         rounded = total.astype(BF16)
         wide_send[...] = rounded
         wide_recv[parity, 0] = rounded
-        order = [blocks // 2] + [b for b in range(1, blocks) if b != blocks // 2]
-        for block in order:
+        middle = blocks // 2
+        sides = [b for b in range(1, blocks) if b != middle]
+
+        def send_wide(block):
+            slot = blocks - block
             remote(
-                wide_send, wide_recv.at[parity, blocks - block], bs_sem, br_sem.at[parity],
+                wide_send, wide_recv.at[parity, slot], bs_sem, br_sem.at[parity, slot],
                 at_pix(block * WINDOW),
             ).start()
 
-        @pl.when(jnp.logical_not(started))
+        def wait_wide(slot):
+            part = wide_recv.at[parity, slot]
+            remote(part, part, bs_sem, br_sem.at[parity, slot], at_pix(1)).wait_recv()
+
+        def send_rows(block):
+            remote(
+                rows_wide.at[parity, 0], rows_wide.at[parity, blocks - block], brs_sem,
+                brr_sem.at[parity], at_pix(block * WINDOW),
+            ).start()
+
+        @pl.when(started)
+        def _():
+            send_wide(middle)
+
+        for block in sides:
+            send_wide(block)
+        part = rows_near.at[pl.ds(0, len(NEAR))]
+        remote(part, part, arr_sem, arr_sem, at_pix(1)).wait_recv()
+        for slot in range(WINDOW):
+            rows_wide[parity, 0, slot] = rows_near[slot]
+        for block in sides:
+            send_rows(block)
+
+        @pl.when(first)
         def _():
             low_part = (total - rounded.astype(F32)).astype(BF16)
             wide_low[...] = low_part
             wide_low_recv[0] = low_part
-            for block in order:
+            wait_wide(early)
+            send_wide(middle)
+            for block in [middle] + sides:
                 remote(
                     wide_low, wide_low_recv.at[blocks - block], bls_sem, blr_sem,
                     at_pix(block * WINDOW),
                 ).start()
 
-        part = rows_near.at[pl.ds(0, len(NEAR))]
-        remote(part, part, arr_sem, arr_sem, at_pix(1)).wait_recv()
-        for slot in range(WINDOW):
-            rows_wide[parity, 0, slot] = rows_near[slot]
-        for block in order:
-            remote(
-                rows_wide.at[parity, 0], rows_wide.at[parity, blocks - block], brs_sem, brr_sem.at[parity],
-                at_pix(block * WINDOW),
-            ).start()
+        send_rows(middle)
 
         @pl.when(started)
         def _():
@@ -204,15 +250,19 @@
         step_row = jnp.where(started, grad_sq / (image_sq + smooth_sq), -1.0)
         step = to_column(step_row, eye)
 
-        part = wide_recv.at[parity, pl.ds(0, blocks - 1)]
-        remote(part, part, bs_sem, br_sem.at[parity], at_pix(1)).wait_recv()
+        @pl.when(started)
+        def _():
+            wait_wide(early)
+
+        wait_wide(blocks - early)
+        wait_wide(middle)
         total = None
         for block in range(blocks):
             term = wide_recv[parity, lax.rem(block - own_block + blocks, blocks)].astype(F32)
             total = term if total is None else total + term
         own_part[...] = total
 
-        @pl.when(jnp.logical_not(started))
+        @pl.when(first)
         def _():
             part = wide_low_recv.at[pl.ds(0, blocks - 1)]
             remote(part, part, bls_sem, blr_sem, at_pix(1)).wait_recv()
@@ -233,38 +283,61 @@
         rounded = grad[...].astype(BF16)
         near_grad[own_class] = rounded
         for offset in NEAR:
-            remote(
-                near_grad.at[own_class], near_grad.at[own_class], cs_sem, cr_sem.at[offset + 3],
-                at_pix(-offset),
-            ).start()
+            if offset == WINDOW // 2:
+                for part, place in enumerate((-offset, offset)):
+                    piece = near_grad.at[own_class, pl.ds(part * half, half)]
+                    remote(piece, piece, cs_sem, cr_sem.at[offset + 3], at_pix(place)).start()
+            else:
+                piece = near_grad.at[own_class]
+                remote(piece, piece, cs_sem, cr_sem.at[offset + 3], at_pix(-offset)).start()
 
         residual[...] = residual[...] - step * image[...]
 
-        def taken(index):
-            block = near_grad[index]
-            value = block.astype(F32)
-            return (
-                lax.dot_general(
-                    block, gmat[index], (((1,), (1,)), ((), ())), preferred_element_type=F32
-                ),
-                value * value,
+        def columns_image(block, index, start, size):
+            return lax.dot_general(
+                block, gmat[index, start : start + size], (((1,), (1,)), ((), ())),
+                preferred_element_type=F32,
             )
 
-        product, squares = taken(own_class)
-        partial[...] = product
-        for offset in (1, -1, 2, -2, 3, -3, 4):
+        block = near_grad[own_class]
+        partial[...] = columns_image(block, own_class, 0, pixels)
+        value = block.astype(F32)
+        squares = value * value
+        my_rows = pl.ds(pl.multiple_of(core * half, half), half)
+        their_rows = pl.ds(pl.multiple_of((1 - core) * half, half), half)
+
+        def pair_copy(index):
+            start, size = parts[index]
+            cut = pl.ds(start, size)
+            return remote(
+                partial.at[their_rows, cut], pair_recv.at[:, cut], xs_sem.at[0, index],
+                x1r_sem.at[index], {"par": mate},
+            )
+
+        def back_copy(index):
+            start, size = parts[index]
+            cut = pl.ds(start, size)
+            return remote(
+                half_send.at[:, cut], half_recv.at[:, cut], xs_sem.at[1, index],
+                x3r_sem.at[index], {"par": mate},
+            )
+
+        arrivals = (1, -1, 2, -2, 3, -3, 4)
+        for offset in arrivals:
+            place = class_at(offset)
             remote(
                 near_grad.at[0], near_grad.at[0], cs_sem, cr_sem.at[offset + 3], at_pix(1)
             ).wait_recv()
-            product, more = taken(class_at(offset))
-            partial[...] += product
-            squares = squares + more
+            block = near_grad[place]
+            if offset == arrivals[-1]:
+                for index, (start, size) in enumerate(parts):
+                    partial[:, start : start + size] += columns_image(block, place, start, size)
+                    pair_copy(index).start()
+            else:
+                partial[...] += columns_image(block, place, 0, pixels)
+            value = block.astype(F32)
+            squares = squares + value * value
         all_par(fresh_rows, row_sums(squares, eye), fr_sem, fs_sem, 0)
-        away = remote(
-            partial.at[pl.ds(pl.multiple_of((1 - core) * half, half), half)], pair_recv,
-            xs_sem.at[0], x1r_sem, {"par": mate},
-        )
-        away.start()
 
         low = remote(near_grad.at[0], halo.at[1], hs_sem.at[0], hr_sem.at[1], {"par": lax.rem(par + n_par - 1, n_par)})
         high = remote(near_grad.at[WINDOW - 1], halo.at[0], hs_sem.at[1], hr_sem.at[0], at_par(1))
@@ -277,19 +350,22 @@
         def _():
             high.start()
 
-        away.wait_recv()
-        mine = partial[pl.ds(pl.multiple_of(core * half, half), half)] + pair_recv[...]
-        chip_buf[parity, chip] = mine.astype(BF16)
-        for offset in (2, 1, 3):
-            remote(
-                chip_buf.at[parity, chip], chip_buf.at[parity, chip], xs_sem.at[1], x2r_sem.at[parity],
-                at_par(2 * offset),
-            ).start()
+        for index, (start, size) in enumerate(parts):
+            cut = slice(start, start + size)
+            pair_copy(index).wait_recv()
+            mine = partial[my_rows, cut] + pair_recv[:, cut]
+            chip_buf[parity, chip, :, cut] = mine.astype(BF16)
+            piece = chip_buf.at[parity, chip, :, pl.ds(start, size)]
+            for offset in (2, 1, 3):
+                remote(
+                    piece, piece, xs_sem.at[2, index], x2r_sem.at[parity, index], at_par(2 * offset)
+                ).start()
 
         wait_rows(fresh_rows, fr_sem, n_par - 1)
         fresh_sq = sum_par(fresh_rows)
         ratio_row = jnp.where(started, fresh_sq / grad_sq, 0.0)
         ratio = to_column(ratio_row, eye)
+        ratio_buf[...] = jnp.broadcast_to(ratio, ratio_buf.shape)
         for row in range(rows):
             old = direction[row + rows_per]
             solution[row] = solution[row] + step * old
@@ -328,23 +404,30 @@
             here, beside = neighbours_sum(smooth1, row + 1)
             smooth2[row] = here - 0.25 * (beside + smooth1[row] + smooth1[row + 2])
 
-        part = chip_buf.at[parity, pl.ds(0, chips - 1)]
-        remote(part, part, xs_sem.at[1], x2r_sem.at[parity], at_par(1)).wait_recv()
-        total = chip_buf[parity, 0].astype(F32)
-        for index in range(1, chips):
-            total = total + chip_buf[parity, index].astype(F32)
-        my_rows = pl.ds(pl.multiple_of(core * half, half), half)
-        their_rows = pl.ds(pl.multiple_of((1 - core) * half, half), half)
-        half_send[...] = total
-        back = remote(half_send, half_recv, xs_sem.at[2], x3r_sem, {"par": mate})
-        back.start()
-        partial[my_rows] = total
-        away.wait_send()
-        back.wait_recv()
-        partial[their_rows] = half_recv[...]
-        value = partial[...] + ratio * image[...]
-        image[...] = value
-        image_bf[...] = value.astype(BF16)
+        def chip_parts(index):
+            start, size = parts[index]
+            return chip_buf.at[parity, pl.ds(0, chips - 1), :, pl.ds(start, size)]
+
+        for index, (start, size) in enumerate(parts):
+            cut = slice(start, start + size)
+            part = chip_parts(index)
+            remote(
+                part, part, xs_sem.at[2, index], x2r_sem.at[parity, index], at_par(1)
+            ).wait_recv()
+            total = chip_buf[parity, 0, :, cut].astype(F32)
+            for other in range(1, chips):
+                total = total + chip_buf[parity, other, :, cut].astype(F32)
+            half_send[:, cut] = total
+            back_copy(index).start()
+            value = total + ratio_buf[my_rows, 0:1] * image[my_rows, cut]
+            image[my_rows, cut] = value
+            image_bf[my_rows, cut] = value.astype(BF16)
+        for index, (start, size) in enumerate(parts):
+            cut = slice(start, start + size)
+            back_copy(index).wait_recv()
+            value = half_recv[:, cut] + ratio_buf[their_rows, 0:1] * image[their_rows, cut]
+            image[their_rows, cut] = value
+            image_bf[their_rows, cut] = value.astype(BF16)
 
         remote(near_send, near_send, as_sem, as_sem, at_pix(1)).wait_send()
         part = rows_near.at[pl.ds(0, len(NEAR))]
@@ -357,9 +440,13 @@
         part = fresh_rows.at[pl.ds(0, n_par - 1)]
         remote(part, part, fs_sem, fs_sem, at_pix(1)).wait_send()
         remote(part, part, ss_sem, ss_sem, at_pix(1)).wait_send()
-        part = chip_buf.at[parity, pl.ds(0, chips - 1)]
-        remote(part, part, xs_sem.at[1], xs_sem.at[1], at_par(1)).wait_send()
-        back.wait_send()
+        for index in range(len(parts)):
+            part = chip_parts(index)
+            remote(
+                part, part, xs_sem.at[2, index], x2r_sem.at[parity, index], at_par(1)
+            ).wait_send()
+            pair_copy(index).wait_send()
+            back_copy(index).wait_send()
 
         @pl.when(par > 0)
         def _():
@@ -470,12 +557,13 @@
                 vmem((n_par, 1, GRID), F32),
                 vmem((n_pix, 1, GRID), F32),
                 vmem((3, 1, GRID), F32),
+                vmem((sets, GRID), F32),
                 dma((WINDOW,)),
                 dma, dma,
-                dma, dma((2,)),
+                dma, dma((2, blocks)),
                 dma, dma((WINDOW,)),
                 dma((2,)), dma((2,)),
-                dma((3,)), dma, dma((2,)), dma,
+                dma((3, 2)), dma((2,)), dma((2, 2)), dma((2,)),
                 dma, dma,
                 dma, dma,
                 dma, dma,

time: 253 us -> 249 us (0.984)
  Pallas kernels: 249 us -> 244 us
    pallas_call x1, Pallas kernels: 249 us -> 244 us  [on_device(): pl.pallas_call(functools.partial(kernel, n_pix, n_par), out_shape=(jax.Sh...]
where the time goes in v2:
time: 249 us; the launch traced here: 248 us
  Pallas kernels  244 us (98%)
  local copies, waits for them, and re-layouts  3.25 us (1%)
    pallas_call x1, Pallas kernels, on_device(): pl.pallas_call(functools.partial(kernel, n_pix, n_par), out_shape=(jax.Sh...  244 us

profile of v2, /device:TPU:33, one launch (start us, length us, event | category | flops | bytes accessed | tf_op | source)
XLA Modules:
  0.0 248.1 jit_solution(8750535038437361313)
XLA Ops:
  0.6 244.2 %shard_map.41 = (f32[32,2048]{1,0:T(8,128)}, f32[32,1152]{1,0:T(8,128)}) custom-call(bf16[1152,2048]{1,0:T(8,128)(2,1)} %green.1, bf16[32,1152]{1,0:T(8,128)(2,1)} %observed.1), custom_call_target="tpu_custom_call" | custom-call | tf_op jit(solution)/shard_map/pallas_call | solution.py:514
  244.8 1.7 copy.6
  246.5 1.6 copy.7
